TPU v7x, 32 devices: a whole 2x2x4 slice. The times are simulated.
32 devices in a mesh: data: 32 (over z, y, x, core).
Axes of the slice: x: 2, y: 2, z: 4, core: 2. Of those that a mesh axis runs over, the one named last changes fastest.
Arguments:
- x_in: bfloat16 [32768, 768], P('data')
- dy_in: bfloat16 [32768, 768], P('data')
- weights: bfloat16 [4, 768, 768], replicated
- a_old: float32 [3072, 768], P('data')
- s_old: float32 [3072, 768], P('data')
- a_inv: float32 [3072, 768], P('data')
- s_inv: float32 [4, 768, 768], replicated
Outputs:
- output 1: float32 [4, 768, 768], replicated
- output 2: float32 [3072, 768], P('data')
- output 3: float32 [3072, 768], P('data')
All inputs are finite; a program needn't handle non-finite values.
Results may differ from a plain program's by a relative error of at most 0.0010606.
Values are sent between devices in bfloat16 or wider.
A program may use at most 1 GiB of HBM per device.

v0:
```python
import functools
import jax
import jax.numpy as jnp
from jax import lax
from jax.sharding import PartitionSpec as P

FACTOR_DECAY = 0.75
PRECISE = lax.Precision.HIGHEST


def gelu_grad(pre_act, d_act):
    pullback = jax.vjp(functools.partial(jax.nn.gelu, approximate=True), pre_act.astype(jnp.float32))[1]
    return pullback(d_act.astype(jnp.float32))[0].astype(jnp.bfloat16)


def cross_rows(left_op, right_op):
    return jnp.einsum("bi,bj->ij", left_op, right_op, preferred_element_type=jnp.float32)


def local_pass(x_loc, dy_loc, weights):
    n_layers = weights.shape[0]
    layer_inputs = [x_loc]
    pre_acts = []
    for layer_id in range(n_layers - 1):
        pre_act = jnp.dot(layer_inputs[layer_id], weights[layer_id], preferred_element_type=jnp.float32).astype(jnp.bfloat16)
        pre_acts.append(pre_act)
        layer_inputs.append(jax.nn.gelu(pre_act.astype(jnp.float32), approximate=True).astype(jnp.bfloat16))
    out_grads = [dy_loc] * n_layers
    for layer_id in range(n_layers - 1, 0, -1):
        d_act = jnp.einsum("bj,ij->bi", out_grads[layer_id], weights[layer_id], preferred_element_type=jnp.float32).astype(jnp.bfloat16)
        out_grads[layer_id - 1] = gelu_grad(pre_acts[layer_id - 1], d_act)
    return layer_inputs, out_grads


def solution(mesh):
    n_dev = mesh.shape["data"]

    def device_step(x_loc, dy_loc, weights, a_old_rows, s_old_rows, a_inv_rows, s_inv):
        n_layers = weights.shape[0]
        model_width = weights.shape[1]
        batch_total = x_loc.shape[0] * n_dev
        layer_inputs, out_grads = local_pass(x_loc, dy_loc, weights)
        a_loc = jnp.concatenate([cross_rows(h_in, h_in) for h_in in layer_inputs], axis=0) / batch_total
        s_loc = jnp.concatenate([cross_rows(g_out, g_out) for g_out in out_grads], axis=0) / batch_total
        w_loc = jnp.stack([cross_rows(h_in, g_out) for h_in, g_out in zip(layer_inputs, out_grads)]) / batch_total
        a_sum = lax.psum_scatter(a_loc, "data", scatter_dimension=0, tiled=True)
        s_sum = lax.psum_scatter(s_loc, "data", scatter_dimension=0, tiled=True)
        w_grad = lax.psum(w_loc, "data")
        own_rows = a_old_rows.shape[0]
        layer_id = (lax.axis_index("data") * own_rows) // model_width
        w_grad_own = lax.dynamic_index_in_dim(w_grad, layer_id, axis=0, keepdims=False)
        s_inv_own = lax.dynamic_index_in_dim(s_inv, layer_id, axis=0, keepdims=False)
        left_prod = jnp.dot(a_inv_rows, w_grad_own, precision=PRECISE)
        u_rows = jnp.dot(left_prod, s_inv_own, precision=PRECISE)
        u_full = lax.all_gather(u_rows, "data", axis=0, tiled=True).reshape(n_layers, model_width, model_width)
        a_new = FACTOR_DECAY * a_old_rows + (1.0 - FACTOR_DECAY) * a_sum
        s_new = FACTOR_DECAY * s_old_rows + (1.0 - FACTOR_DECAY) * s_sum
        return u_full, a_new, s_new

    row_spec = P("data", None)
    return jax.shard_map(
        device_step,
        mesh=mesh,
        in_specs=(row_spec, row_spec, P(), row_spec, row_spec, row_spec, P()),
        out_specs=(P(), row_spec, row_spec),
        check_vma=False,
    )
```

profile of v0, /device:TPU:0, one launch (start us, length us, event | category | flops | bytes accessed | tf_op | source)
XLA Modules:
  0.0 612.5 jit_solution(7845548859921639945)
XLA Ops:
  7.2 0.0 copy-start
  7.2 0.0 all-reduce.2.cloned.1.call-start
  7.2 3.3 convolution_convert_fusion.4
  10.5 2.1 convolution_convert_fusion.3
  12.6 0.0 copy-start.13
  12.6 2.1 convolution_convert_fusion.2
  14.7 3.7 fusion.5
  18.5 3.6 fusion.8
  22.0 3.5 fusion.11
  25.6 1.8 convolution_bitcast_fusion.2
  27.4 0.0 copy-done.13
  27.5 0.0 copy-done.6
  27.5 1.9 convolution_bitcast_fusion.1
  29.3 0.0 copy-done.15
  29.3 0.0 copy-start.5
  29.4 1.8 convolution_bitcast_fusion
  31.2 1.4 convolution_bitcast_fusion.3
  32.6 4.2 maximum_multiply_fusion
  36.8 0.0 all-reduce.2.cloned.1.call-update
  36.9 0.3 reduce-scatter.5.cloned.1.call-start
  37.1 3.5 fusion.65
  40.6 1.5 fusion.66
  42.1 1.5 fusion.67
  43.6 1.5 fusion.68
  45.0 3.9 maximum_multiply_fusion.2
  49.0 0.0 reduce-scatter.5.cloned.1.call-update
  49.0 0.0 reduce-scatter.3.cloned.1.call-start
  49.0 1.5 fusion.64
  50.5 0.0 copy-done.16
  50.5 0.0 copy-start.14
  50.5 2.6 fusion.53
  53.2 2.6 fusion.56
  55.8 2.6 fusion.60
  58.5 4.0 maximum_multiply_fusion.1
  62.5 0.0 reduce-scatter.3.cloned.1.call-update
  62.5 0.3 all-gather.2.cloned.1.call-start
  62.8 0.0 copy-start.2
  62.8 0.0 copy-start.3
  62.9 167.2 %all-reduce.2.cloned.1.call-done = f32[4,768,768]{1,2,0:T(8,128)} async-done(((f32[4,768,768]{1,2,0:T(8,128)}), f32[4,768,768]{1,2,0:T(8,128)}) %all-reduce.2.cloned.1.call-update) | async-done | bytes 9437200 | tf_op jit(solution)/shard_map/psum | solution.py:48
  230.1 3.6 fusion.35
  233.7 3.9 fusion.33
  237.6 0.0 all-gather.2.cloned.1.call-update
  237.6 134.7 %reduce-scatter.5.cloned.1.call-done = f32[96,768]{1,0:T(8,128)} async-done(((f32[3072,768]{1,0:T(8,128)}), f32[96,768]{1,0:T(8,128)}) %reduce-scatter.5.cloned.1.call-update) | async-done | bytes 294928 | tf_op jit(solution)/shard_map/reduce_scatter | solution.py:47
  372.3 1.7 multiply_add_fusion
  374.0 139.5 %reduce-scatter.3.cloned.1.call-done = f32[96,768]{1,0:T(8,128)} async-done(((f32[3072,768]{1,0:T(8,128)}), f32[96,768]{1,0:T(8,128)}) %reduce-scatter.3.cloned.1.call-update) | async-done | bytes 294928 | tf_op jit(solution)/shard_map/reduce_scatter | solution.py:46
  513.5 1.7 multiply_add_fusion.1
  515.2 82.3 %all-gather.2.cloned.1.call-done = f32[3072,768]{1,0:T(8,128)} async-done(((f32[96,768]{1,0:T(8,128)}), f32[3072,768]{1,0:T(8,128)}) %all-gather.2.cloned.1.call-update) | async-done | bytes 9437200 | tf_op jit(solution)/shard_map/all_gather | solution.py:55
  597.5 8.0 %copy.18 = f32[4,768,768]{2,1,0:T(8,128)} copy(f32[4,768,768]{2,1,0:T(8,128)} %bitcast.54) | data formatting | bytes 18874368
  (24 shorter events, 0.0 us)
Async XLA Ops:
  7.2 7.6 %copy-start = (bf16[1024,768]{1,0:T(8,128)(2,1)S(1)}, bf16[1024,768]{1,0:T(8,128)(2,1)}, u32[]{:S(2)}) copy-start(bf16[1024,768]{1,0:T(8,128)(2,1)} %param.8) | copy-start | bytes 4718596
  7.2 222.9 %all-reduce.2.cloned.1.call-start = ((), (), s32[]{:S(2)}) async-start(), calls=%async_computation.2 | async-start | bytes 18874368 | tf_op jit(solution)/shard_map/psum | solution.py:48
  7.2 3.3 copy-start.4
  10.5 15.1 %copy-start.11 = (bf16[1024,768]{1,0:T(8,128)(2,1)}, bf16[1024,768]{1,0:T(8,128)(2,1)S(1)}, u32[]{:S(2)}) copy-start(bf16[1024,768]{1,0:T(8,128)(2,1)S(1)} %convolution_convert_fusion.4) | copy-start | bytes 4718596
  12.6 14.8 %copy-start.13 = (bf16[1024,768]{1,0:T(8,128)(2,1)}, bf16[1024,768]{1,0:T(8,128)(2,1)S(1)}, u32[]{:S(2)}) copy-start(bf16[1024,768]{1,0:T(8,128)(2,1)S(1)} %convolution_convert_fusion.3) | copy-start | bytes 4718596
  14.7 14.6 %copy-start.15 = (bf16[1024,768]{1,0:T(8,128)(2,1)}, bf16[1024,768]{1,0:T(8,128)(2,1)S(1)}, u32[]{:S(2)}) copy-start(bf16[1024,768]{1,0:T(8,128)(2,1)S(1)} %convolution_convert_fusion.2) | copy-start | bytes 4718596
  18.5 9.0 %copy-start.6 = (bf16[1024,768]{1,0:T(8,128)(2,1)}, bf16[1024,768]{1,0:T(8,128)(2,1)S(1)}, u32[]{:S(2)}) copy-start(bf16[1024,768]{1,0:T(8,128)(2,1)S(1)} %fusion.5) | copy-start | bytes 4718596
  22.0 3.6 copy-start.8
  25.6 5.6 copy-start.10
  29.3 1.8 copy-start.5
  36.9 335.4 %reduce-scatter.5.cloned.1.call-start = ((), (), s32[]{:S(2)}) async-start(), calls=%async_computation.5 | async-start | bytes 9732096 | tf_op jit(solution)/shard_map/reduce_scatter | solution.py:47
  37.1 3.5 copy-start.9
  40.6 1.5 copy-start.7
  49.0 464.5 %reduce-scatter.3.cloned.1.call-start = ((), (), s32[]{:S(2)}) async-start(), calls=%async_computation.4 | async-start | bytes 9732096 | tf_op jit(solution)/shard_map/reduce_scatter | solution.py:46
  49.0 1.5 copy-start.16
  50.5 2.6 copy-start.14
  53.2 2.7 copy-start.12
  62.5 167.6 %copy-start.1 = (f32[96,768]{1,0:T(8,128)S(1)}, f32[96,768]{1,0:T(8,128)}, u32[]{:S(2)}) copy-start(f32[96,768]{1,0:T(8,128)} %param.12) | copy-start | bytes 884740
  62.5 535.0 %all-gather.2.cloned.1.call-start = ((), (), s32[]{:S(2)}) async-start(), calls=%async_computation.3 | async-start | bytes 9732096 | tf_op jit(solution)/shard_map/all_gather | solution.py:55
  62.8 309.5 %copy-start.2 = (f32[96,768]{1,0:T(8,128)S(1)}, f32[96,768]{1,0:T(8,128)}, u32[]{:S(2)}) copy-start(f32[96,768]{1,0:T(8,128)} %param.11) | copy-start | bytes 884740
  62.8 450.6 %copy-start.3 = (f32[96,768]{1,0:T(8,128)S(1)}, f32[96,768]{1,0:T(8,128)}, u32[]{:S(2)}) copy-start(f32[96,768]{1,0:T(8,128)} %param.10) | copy-start | bytes 884740
Sparse Core Ops, SparseCore 0:
  37.0 193.0 all-reduce.1
  236.0 136.2 reduce-scatter.4
  378.2 135.2 reduce-scatter.2
  516.8 80.6 all-gather.1
where the time goes:
time: 617 us; the launch traced here: 613 us
  waiting for transfers between devices  524 us (85%)
  matrix products  49.9 us (8%)
  other arithmetic  15.6 us (3%)
  between operations  14.6 us (2%)
  local copies, waits for them, and re-layouts  8.11 us (1%)
    psum x1, waiting for transfers between devices, device_step(): w_grad = lax.psum(w_loc, 'data')  167 us
    reduce_scatter x1, waiting for transfers between devices, device_step(): a_sum = lax.psum_scatter(a_loc, 'data', scatter_dimension=0, tiled=True)  139 us
    reduce_scatter x1, waiting for transfers between devices, device_step(): s_sum = lax.psum_scatter(s_loc, 'data', scatter_dimension=0, tiled=True)  135 us
    all_gather x1, waiting for transfers between devices, device_step(): lax.all_gather(u_rows, 'data', axis=0, tiled=True)  82.3 us
    dot_general x12, matrix products, cross_rows(): jnp.einsum('bi,bj->ij', left_op, right_op, preferred_element_type=jnp.flo...  24.1 us
  transfers between devices with their start and end apart: 4, of which 4 were waited for; matrix products, arithmetic and copies ran while one was open for 6% of the time, Pallas kernels for 0%

commit v1 on v0

v1 whole, which is shorter than its diff:
```python
import math
import jax
import jax.numpy as jnp
from jax import lax
from jax.experimental import pallas as pl
from jax.experimental.pallas import tpu as pltpu
from jax.sharding import PartitionSpec as P

DECAY = 0.75
F32 = jnp.float32
BF16 = jnp.bfloat16
MESH = pl.DeviceIdType.MESH
HIGH = lax.Precision.HIGHEST
LAYERS = 4
D = 768
ROWS = 1024
OWN = 96
HALF = 384
GELU_C = math.sqrt(2.0 / math.pi)
NT = (((1,), (1,)), ((), ()))

STEPS = 2560.0
BASE = 21.0
PAIR = OWN // 2
CODE = OWN + PAIR


def encode(v):
    hi = v.astype(BF16)
    h = hi.astype(F32)
    q = jnp.round((v - h) / jnp.where(h == 0.0, 1.0, h) * STEPS)
    q = jnp.clip(q, -10.0, 10.0)
    lo = q[:PAIR] * BASE + q[PAIR:]
    return hi, lo.astype(BF16)


def decode(hi, lo):
    h = hi.astype(F32)
    w = lo.astype(F32)
    top = jnp.round(w * (1.0 / BASE))
    q = jnp.concatenate([top, w - BASE * top], axis=-2)
    return h + h * (q * (1.0 / STEPS))


def put(ref, idx, v):
    hi, lo = encode(v)
    ref[(*idx, slice(0, OWN))] = hi
    ref[(*idx, slice(OWN, CODE))] = lo


def get(ref, idx):
    return decode(ref[(*idx, slice(0, OWN))], ref[(*idx, slice(OWN, CODE))])


def gelu_tanh(v):
    return jnp.tanh(GELU_C * (v + 0.044715 * (v * v * v)))


F, B, W, PR, T, C, Z, R, U, Y, V, AS = range(12)
EVENTS = [
    (F, 0), (W, 0), (PR, 4), (F, 1), (W, 7), (PR, 11), (F, 2), (W, 1), (PR, 5), (T, 4),
    (B, 3), (W, 3), (PR, 3), (B, 2), (W, 6), (W, 2), (PR, 2), (T, 11), (B, 1), (W, 5), (PR, 1), (T, 5), (C, 4),
    (W, 4), (PR, 0), (T, 3), (C, 11), (T, 2), (C, 5), (PR, 6), (C, 3), (T, 1), (C, 2), (T, 0), (PR, 7),
    (C, 1), (C, 0), (PR, 10), (Z, 0), (T, 6), (T, 7), (R, 0), (PR, 9), (PR, 8), (T, 10), (C, 6), (C, 7),
    (U, 0), (T, 9), (T, 8), (C, 10), (Y, 1), (V, 0), (Y, 2), (Y, 3), (C, 9), (C, 8), (V, 1), (V, 2), (V, 3), (AS, 0),
]


def kernel(
    x_hbm, dy_hbm, wt_hbm, w_hbm, sinv_hbm, a_old, s_old, a_inv,
    u_out, a_new, s_new,
    hg, wbuf, lhs, acc, accx, s1, r1, r2, zr, gcode, gfull, sinv, ubuf,
    lsem, wsem, d2d_s, d2d_r, s1_s, s1_r, s2_s, s2_r, z_s, z_r, g_s, g_r, uz_s, uz_r, u_s, u_r, us_loc,
):
    me = lax.axis_index("data")
    c = me % 2
    x = (me // 2) % 2
    y = (me // 4) % 2
    z = me // 8
    mate = me + 1 - 2 * c
    x_nbr = me + 2 - 4 * x
    y_nbr = me + 4 - 8 * y
    z_peer = [(me + 8 * k) % 32 for k in range(4)]

    def row_block(dy_, dx_):
        return 4 * ((y + dy_) % 2) + 2 * ((x + dx_) % 2) + c

    blocks = [row_block(0, 0), row_block(0, 1), row_block(1, 0), row_block(1, 1)]

    def rcopy(src, dst, ss, rs, dev):
        return pltpu.make_async_remote_copy(
            src_ref=src, dst_ref=dst, send_sem=ss, recv_sem=rs, device_id=(dev,), device_id_type=MESH
        )

    own = pl.ds(0, ROWS)
    far = pl.ds(ROWS, ROWS)
    ld_x = pltpu.make_async_copy(x_hbm, hg.at[0, :, own], lsem.at[0])
    ld_dy = pltpu.make_async_copy(dy_hbm, hg.at[7, :, own], lsem.at[1])
    ld_si = pltpu.make_async_copy(sinv_hbm.at[z], sinv, lsem.at[2])
    ld_x.start()
    ld_dy.start()
    for l in range(3):
        pltpu.make_async_copy(wt_hbm.at[l], wbuf.at[l], wsem.at[l]).start()
    ld_si.start()

    barrier = pltpu.get_barrier_semaphore()
    for dev in (mate, x_nbr, y_nbr, z_peer[1], z_peer[2], z_peer[3]):
        pl.semaphore_signal(barrier, inc=1, device_id=(dev,), device_id_type=MESH)
    pl.semaphore_wait(barrier, 6)

    def share(n):
        return rcopy(hg.at[n, :, own], hg.at[n, :, far], d2d_s.at[n], d2d_r.at[n], mate)

    def forward(l):
        pltpu.make_async_copy(wt_hbm.at[l], wbuf.at[l], wsem.at[l]).wait()

        @pl.loop(0, 3)
        def _(i):
            rows = pl.ds(pl.multiple_of(i * 256, 256), 256)
            pre = jnp.dot(wbuf[l, rows, :], hg[l, :, own], preferred_element_type=F32).astype(BF16)
            hg[4 + l, rows, own] = pre
            v = pre.astype(F32)
            hg[l + 1, rows, own] = (v * (0.5 * (1.0 + gelu_tanh(v)))).astype(BF16)

        share(l + 1).start()
        pltpu.make_async_copy(w_hbm.at[3 - l], wbuf.at[l], wsem.at[l]).start()

    def backward(l):
        k = 3 - l
        pltpu.make_async_copy(w_hbm.at[l], wbuf.at[k], wsem.at[k]).wait()

        @pl.loop(0, 3)
        def _(i):
            rows = pl.ds(pl.multiple_of(i * 256, 256), 256)
            dh = jnp.dot(wbuf[k, rows, :], hg[4 + l, :, own], preferred_element_type=F32).astype(BF16).astype(F32)
            v = hg[3 + l, rows, own].astype(F32)
            t = gelu_tanh(v)
            slope = 0.5 * (1.0 + t) + (0.5 * v) * (1.0 - t * t) * (GELU_C * (1.0 + (3.0 * 0.044715) * (v * v)))
            hg[3 + l, rows, own] = (dh * slope).astype(BF16)

        share(3 + l).start()

    def st1(m, j):
        return rcopy(s1.at[m, j], r1.at[m, j], s1_s.at[m, j], s1_r.at[m, j], (x_nbr, y_nbr)[j])

    def st2(m, j):
        return rcopy(s1.at[m, 0, j], r2.at[m, j], s2_s.at[m, j], s2_r.at[m, j], (y_nbr, x_nbr)[j])

    def product(m):
        kind = m // 4
        l = m % 4
        left = jnp.where(kind == 2, 4 + l, l)
        right = jnp.where(kind == 1, l, 4 + l)
        for d in range(4):
            lhs[pl.ds(OWN * d, OWN), :] = hg[left, pl.ds(pl.multiple_of(blocks[d] * OWN, OWN), OWN), :]

        @pl.loop(0, 2)
        def _(j):
            cols = pl.ds(pl.multiple_of(j * HALF, HALF), HALF)
            out = lax.dot_general(lhs[...], hg[right, cols, :], NT, preferred_element_type=F32)
            acc[m, :, cols] = out[0:OWN]
            first = out[OWN : 2 * OWN]
            second = out[2 * OWN : 3 * OWN]
            put(s1, (m, j, 0), jnp.where(j == 0, first, second))
            accx[m, j] = jnp.where(j == 0, second, first)
            put(s1, (m, j, 1), out[3 * OWN :])

        for j in range(2):
            st1(m, j).start()

    def turn(m):
        st1(m, 0).wait_send()
        for j in range(2):
            st1(m, j).wait_recv()
            put(s1, (m, 0, j), accx[m, j] + get(r1, (m, j, 1)))
            st2(m, j).start()
            acc[m, :, pl.ds(j * HALF, HALF)] += get(r1, (m, j, 0))

    def z_copy(m):
        kind = m // 4
        l = m % 4
        slot = (l - z + 3) % 4
        return rcopy(s1.at[m, 1], zr.at[kind, slot], z_s.at[m], z_r.at[kind, slot], (me + 8 * (l - z) + 32) % 32)

    def across(m):
        st1(m, 1).wait_send()
        for j in range(2):
            st2(m, j).wait_recv()
            total = acc[m, :, pl.ds(j * HALF, HALF)] + get(r2, (m, j))
            acc[m, :, pl.ds(j * HALF, HALF)] = total

            @pl.when(m % 4 != z)
            def _():
                put(s1, (m, 1, j), total)

        @pl.when(m % 4 != z)
        def _():
            z_copy(m).start()

    def z_total(kind, j):
        t = acc[kind * 4 + z, :, pl.ds(j * HALF, HALF)]
        for k in range(3):
            t = t + get(zr, (kind, k, j))
        return t

    def z_wait(kind):
        for k in range(3):
            rcopy(s1.at[0, 1], zr.at[kind, k], z_s.at[0], z_r.at[kind, k], z_peer[k + 1]).wait_recv()

    inv_batch = 1.0 / (ROWS * 32)

    def gather_copies(ref, base, ss, rs, own_src):
        def at(rb, half=None):
            return ref.at[base + rb] if half is None else ref.at[base + rb, half]

        first = [
            rcopy(own_src, at(blocks[0]), ss.at[0], rs.at[0], x_nbr),
            rcopy(own_src, at(blocks[0]), ss.at[1], rs.at[1], y_nbr),
            rcopy(own_src, at(blocks[0]), ss.at[2], rs.at[2], mate),
        ]
        from_x = [
            rcopy(at(blocks[1], 0), at(blocks[1], 0), ss.at[3], rs.at[3], y_nbr),
            rcopy(at(blocks[1]), at(blocks[1]), ss.at[5], rs.at[5], mate),
        ]
        from_y = [
            rcopy(at(blocks[2], 1), at(blocks[2], 1), ss.at[4], rs.at[4], x_nbr),
            rcopy(at(blocks[2]), at(blocks[2]), ss.at[6], rs.at[6], mate),
        ]
        last = rcopy(at(blocks[3]), at(blocks[3]), ss.at[7], rs.at[7], mate)
        return first, from_x, from_y, last

    def gather_rest(copies):
        first, from_x, from_y, last = copies
        first[0].wait_recv()
        for cp in from_x:
            cp.start()
        first[1].wait_recv()
        for cp in from_y:
            cp.start()
        from_x[0].wait_recv()
        from_y[0].wait_recv()
        last.start()

    def gather_end(copies):
        first, from_x, from_y, last = copies
        for cp in (first[2], from_x[1], from_y[1], last):
            cp.wait_recv()

    def gather_sent(copies):
        first, from_x, from_y, last = copies
        for cp in (*first, *from_x, *from_y, last):
            cp.wait_send()

    g_copies = gather_copies(gcode, 0, g_s, g_r, gcode.at[blocks[0]])

    def u_row(l):
        return u_out.at[l * 8 + blocks[0]]

    def u_copies(k):
        l = (z - k + 4) % 4
        return gather_copies(u_out, l * 8, u_s.at[k], u_r.at[k], u_row(l))

    own_first = gather_copies(u_out, z * 8, u_s.at[0], u_r.at[0], ubuf)[0]
    local = pltpu.make_async_copy(ubuf, u_row(z), us_loc)

    def z_send(k, l):
        return rcopy(ubuf, u_row(l), uz_s.at[k - 1], uz_r.at[k - 1], (me + 8 * k) % 32)

    def own_grad(_):
        z_wait(0)
        for j in range(2):
            put(gcode, (blocks[0], j), z_total(0, j) * inv_batch)
        for cp in g_copies[0]:
            cp.start()

    def precondition(_):
        gather_end(g_copies)

        @pl.loop(0, 8)
        def _(b):
            for j in range(2):
                gfull[pl.ds(pl.multiple_of(b * OWN, OWN), OWN), pl.ds(j * HALF, HALF)] = get(gcode, (b, j))

        ld_si.wait()
        left_prod = jnp.dot(a_inv[...], gfull[...], precision=HIGH, preferred_element_type=F32)
        u_rows = jnp.dot(left_prod, sinv[...], precision=HIGH, preferred_element_type=F32)
        for j in range(2):
            put(ubuf, (j,), u_rows[:, j * HALF : (j + 1) * HALF])
        for k in range(1, 4):
            z_send(k, z).start()
        for cp in own_first:
            cp.start()
        local.start()

    def from_plane(k):
        z_send(k, (z - k + 4) % 4).wait_recv()
        for cp in u_copies(k)[0]:
            cp.start()

    def factors(_):
        for kind, old, new in ((1, a_old, a_new), (2, s_old, s_new)):
            z_wait(kind)
            for j in range(2):
                cols = pl.ds(j * HALF, HALF)
                new[:, cols] = DECAY * old[:, cols] + ((1.0 - DECAY) * inv_batch) * z_total(kind, j)

    ld_x.wait()
    share(0).start()
    ld_dy.wait()
    share(7).start()

    actions = {
        F: forward,
        B: backward,
        W: lambda n: share(n).wait_recv(),
        PR: product,
        T: turn,
        C: across,
        Z: own_grad,
        R: lambda _: gather_rest(g_copies),
        U: precondition,
        Y: from_plane,
        V: lambda k: gather_rest(u_copies(k)),
        AS: factors,
    }

    @pl.loop(0, len(EVENTS))
    def _(step):
        code = jnp.int32(0)
        for s, (op, arg) in enumerate(EVENTS):
            code = jnp.where(step == s, op * 16 + arg, code)
        op = code // 16
        arg = code % 16
        for o, act in actions.items():

            @pl.when(op == o)
            def _(act=act):
                act(arg)

    @pl.loop(0, 4)
    def _(k):
        gather_end(u_copies(k))
        gather_sent(u_copies(k))

    for k in range(1, 4):
        z_send(k, z).wait_send()
    local.wait()
    gather_sent(g_copies)

    @pl.loop(0, 8)
    def _(n):
        share(n).wait_send()

    @pl.loop(0, 12)
    def _(m):
        for j in range(2):
            st2(m, j).wait_send()

        @pl.when(m % 4 != z)
        def _():
            z_copy(m).wait_send()


def open_rows(code, rows):
    for b in range(4):
        for j in range(2):
            rows[0, b * OWN : (b + 1) * OWN, j * HALF : (j + 1) * HALF] = get(code, (b, j))


def solution(mesh):
    def device_step(x_loc, dy_loc, weights, a_old_rows, s_old_rows, a_inv_rows, s_inv):
        any_spec = pl.BlockSpec(memory_space=pl.ANY)
        vmem = pl.BlockSpec(memory_space=pltpu.VMEM)
        dma = pltpu.SemaphoreType.DMA
        u_code, a_new, s_new = pl.pallas_call(
            kernel,
            out_shape=(
                jax.ShapeDtypeStruct((LAYERS * 8, 2, CODE, HALF), BF16),
                jax.ShapeDtypeStruct((OWN, D), F32),
                jax.ShapeDtypeStruct((OWN, D), F32),
            ),
            in_specs=[any_spec] * 5 + [vmem] * 3,
            out_specs=(any_spec, vmem, vmem),
            scratch_shapes=[
                pltpu.VMEM((2 * LAYERS, D, 2 * ROWS), BF16),
                pltpu.VMEM((3, D, D), BF16),
                pltpu.VMEM((4 * OWN, 2 * ROWS), BF16),
                pltpu.VMEM((12, OWN, D), F32),
                pltpu.VMEM((12, 2, OWN, HALF), F32),
                pltpu.VMEM((12, 2, 2, CODE, HALF), BF16),
                pltpu.VMEM((12, 2, 2, CODE, HALF), BF16),
                pltpu.VMEM((12, 2, CODE, HALF), BF16),
                pltpu.VMEM((3, 3, 2, CODE, HALF), BF16),
                pltpu.VMEM((8, 2, CODE, HALF), BF16),
                pltpu.VMEM((D, D), F32),
                pltpu.VMEM((D, D), F32),
                pltpu.VMEM((2, CODE, HALF), BF16),
                dma((3,)),
                dma((3,)),
                dma((8,)), dma((8,)),
                dma((12, 2)), dma((12, 2)),
                dma((12, 2)), dma((12, 2)),
                dma((12,)), dma((3, 3)),
                dma((8,)), dma((8,)),
                dma((3,)), dma((3,)),
                dma((4, 8)), dma((4, 8)),
                dma,
            ],
            compiler_params=pltpu.CompilerParams(
                collective_id=0, has_side_effects=True, vmem_limit_bytes=67_000_000
            ),
        )(x_loc.T, dy_loc.T, jnp.swapaxes(weights[:3], 1, 2), weights, s_inv, a_old_rows, s_old_rows, a_inv_rows)
        u_pre = pl.pallas_call(
            open_rows,
            out_shape=jax.ShapeDtypeStruct((LAYERS, D, D), F32),
            grid=(8,),
            in_specs=[pl.BlockSpec((4, 2, CODE, HALF), lambda i: (i, 0, 0, 0))],
            out_specs=pl.BlockSpec((1, 4 * OWN, D), lambda i: (i // 2, i % 2, 0)),
        )(u_code)
        return u_pre, a_new, s_new

    row_spec = P("data", None)
    return jax.shard_map(
        device_step,
        mesh=mesh,
        in_specs=(row_spec, row_spec, P(), row_spec, row_spec, row_spec, P()),
        out_specs=(P(), row_spec, row_spec),
        check_vma=False,
    )
```

time: 617 us -> 188 us (0.30)
  waiting for transfers between devices: 524 us -> 0 us
  Pallas kernels: 0 us -> 172 us
  matrix products: 49.9 us -> 0 us
  other arithmetic: 15.6 us -> 0 us
  between operations: 14.6 us -> 0.67 us
    reduce_scatter x2 -> x0, waiting for transfers between devices: 274 us -> none  [the longest x1 139 us: device_step(): a_sum = lax.psum_scatter(a_loc, 'data', scatter_dimension=0, tiled=True)]
    pallas_call x0 -> x2, Pallas kernels: none -> 172 us  [the longest x1 163 us: device_step(): pl.pallas_call(kernel, out_shape=(jax.ShapeDtypeStruct((LAYERS * 8, 2, CO...]
    psum x1 -> x0, waiting for transfers between devices: 167 us -> none  [device_step(): w_grad = lax.psum(w_loc, 'data')]
    all_gather x1 -> x0, waiting for transfers between devices: 82.3 us -> none  [device_step(): lax.all_gather(u_rows, 'data', axis=0, tiled=True)]
    dot_general x20 -> x0, matrix products: 49.9 us -> none  [the longest x12 24.1 us: cross_rows(): jnp.einsum('bi,bj->ij', left_op, right_op, preferred_element_type=jnp.flo...]
    div x3 -> x0, other arithmetic: 12.1 us -> none  [the longest x1 4.19 us: device_step(): jnp.stack([cross_rows(h_in, g_out) for h_in, g_out in zip(layer_inputs, o...]
  transfers between devices with their start and end apart: 4 -> 0, of which waited for: 4 -> 0; matrix products, arithmetic and copies ran while one was open for 6% -> 0% of each run, Pallas kernels for 0% -> 0%
where the time goes in v1:
time: 188 us; the launch traced here: 185 us
  Pallas kernels  172 us (91%)
  local copies, waits for them, and re-layouts  11.6 us (6%)
    pallas_call x1, Pallas kernels, device_step(): pl.pallas_call(kernel, out_shape=(jax.ShapeDtypeStruct((LAYERS * 8, 2, CO...  163 us
    unnamed x11, local copies, waits for them, and re-layouts  9.57 us
    pallas_call x1, Pallas kernels, device_step(): pl.pallas_call(open_rows, out_shape=jax.ShapeDtypeStruct((LAYERS, D, D),...  9.5 us

profile of v1, /device:TPU:0, one launch (start us, length us, event | category | flops | bytes accessed | tf_op | source)
XLA Modules:
  0.0 184.5 jit_solution(892392994829009)
XLA Ops:
  0.6 0.0 copy-start
  0.6 2.8 %copy.10 = bf16[1024,768]{0,1:T(8,128)(2,1)} copy(bf16[1024,768]{1,0:T(8,128)(2,1)} %param.7) | data formatting | bytes 3145728 | tf_op args[0]
  3.4 0.0 copy-done
  3.4 1.7 copy.11
  5.1 0.0 slice-start
  5.1 2.0 %slice-done = bf16[3,768,768]{2,1,0:T(8,128)(2,1)S(1)} async-done(((bf16[4,768,768]{2,1,0:T(8,128)(2,1)}), bf16[3,768,768]{2,1,0:T(8,128)(2,1)S(1)}, s32[]{:S(2)}) %slice-start) | async-done | bytes 3538968 | tf_op jit(solution)/shard_map/slice | solution.py:412
  7.1 3.7 %copy.13 = bf16[3,768,768]{1,2,0:T(8,128)(2,1)} copy(bf16[3,768,768]{2,1,0:T(8,128)(2,1)S(1)} %slice-done) | data formatting | bytes 7077888
  10.8 162.8 %shard_map.94 = (bf16[32,2,144,384]{3,2,1,0:T(8,128)(2,1)}, f32[96,768]{1,0:T(8,128)}, f32[96,768]{1,0:T(8,128)}) custom-call(bf16[768,1024]{1,0:T(8,128)(2,1)} %bitcast.4, bf16[768,1024]{1,0:T(8,128)(2,1)} %bitcast.5, bf16[3,768,768]{2,1,0:T(8,128)(2,1)} %bitcast.3, bf16[4,768,768]{2,1,0:T(8,128)(2,1)} %w_hbm.1, f32[4,768,768]{2,1,0:T(8,128)} %sinv_hbm.1, ...), custom_call_target="tpu_custom_call" | custom-call | tf_op jit(solution)/shard_map/pallas_call | solution.py:375
  173.6 0.0 copy-start.2
  173.6 0.0 copy-start.1
  173.6 9.5 %shard_map.95 = f32[4,768,768]{2,1,0:T(8,128)} custom-call(bf16[32,2,144,384]{3,2,1,0:T(8,128)(2,1)} %get-tuple-element.6.code), custom_call_target="tpu_custom_call" | custom-call | tf_op jit(solution)/shard_map/pallas_call | solution.py:413
  183.1 0.0 copy-done.2
  183.1 0.7 copy.16
  183.8 0.0 copy-done.1
  183.8 0.7 copy.17
Async XLA Ops:
  0.6 2.8 %copy-start = (bf16[1024,768]{1,0:T(8,128)(2,1)S(1)}, bf16[1024,768]{1,0:T(8,128)(2,1)}, u32[]{:S(2)}) copy-start(bf16[1024,768]{1,0:T(8,128)(2,1)} %param.8) | copy-start | bytes 4718596
  5.1 2.0 %slice-start = ((bf16[4,768,768]{2,1,0:T(8,128)(2,1)}), bf16[3,768,768]{2,1,0:T(8,128)(2,1)S(1)}, s32[]{:S(2)}) async-start(bf16[4,768,768]{2,1,0:T(8,128)(2,1)} %w_hbm.1), calls=%async_computation | async-start | bytes 7077888 | tf_op jit(solution)/shard_map/slice | solution.py:412
  173.6 9.5 %copy-start.2 = (f32[96,768]{1,0:T(8,128)S(1)}, f32[96,768]{1,0:T(8,128)}, u32[]{:S(2)}) copy-start(f32[96,768]{1,0:T(8,128)} %get-tuple-element.13) | copy-start | bytes 884740
  173.6 10.2 %copy-start.1 = (f32[96,768]{1,0:T(8,128)S(1)}, f32[96,768]{1,0:T(8,128)}, u32[]{:S(2)}) copy-start(f32[96,768]{1,0:T(8,128)} %get-tuple-element.14) | copy-start | bytes 884740

commit v2 on v1

--- a/solution.py
+++ b/solution.py
@@ -56,13 +56,15 @@
     return jnp.tanh(GELU_C * (v + 0.044715 * (v * v * v)))
 
 
-F, B, W, PR, T, C, Z, R, U, Y, V, AS = range(12)
+F, B, W, PR, T, C, Z, R, U, Y, V, AS, RQ, VQ = range(14)
 EVENTS = [
-    (F, 0), (W, 0), (PR, 4), (F, 1), (W, 7), (PR, 11), (F, 2), (W, 1), (PR, 5), (T, 4),
-    (B, 3), (W, 3), (PR, 3), (B, 2), (W, 6), (W, 2), (PR, 2), (T, 11), (B, 1), (W, 5), (PR, 1), (T, 5), (C, 4),
-    (W, 4), (PR, 0), (T, 3), (C, 11), (T, 2), (C, 5), (PR, 6), (C, 3), (T, 1), (C, 2), (T, 0), (PR, 7),
-    (C, 1), (C, 0), (PR, 10), (Z, 0), (T, 6), (T, 7), (R, 0), (PR, 9), (PR, 8), (T, 10), (C, 6), (C, 7),
-    (U, 0), (T, 9), (T, 8), (C, 10), (Y, 1), (V, 0), (Y, 2), (Y, 3), (C, 9), (C, 8), (V, 1), (V, 2), (V, 3), (AS, 0),
+    (F, 0), (W, 0), (PR, 4), (W, 7), (PR, 11), (W, 1), (PR, 5), (F, 1), (F, 2), (T, 4),
+    (B, 3), (B, 2), (T, 5), (W, 5), (PR, 1), (W, 3), (PR, 3), (C, 5), (W, 2), (W, 6),
+    (PR, 2), (T, 1), (B, 1), (T, 3), (W, 4), (PR, 0), (T, 2), (C, 3), (T, 0), (C, 1),
+    (PR, 6), (C, 2), (T, 11), (PR, 9), (C, 0), (T, 6), (T, 9), (C, 6), (Z, 0), (C, 11),
+    (C, 4), (R, 0), (PR, 8), (PR, 10), (RQ, 0), (U, 0), (T, 10), (PR, 7), (T, 8), (T, 7),
+    (C, 10), (Y, 1), (C, 7), (C, 8), (C, 9), (Y, 2), (V, 1), (Y, 3), (V, 2), (V, 0),
+    (V, 3), (VQ, 0), (VQ, 2), (VQ, 1), (VQ, 3), (AS, 0),
 ]
 
 
@@ -237,6 +239,9 @@
         first[1].wait_recv()
         for cp in from_y:
             cp.start()
+
+    def gather_last(copies):
+        first, from_x, from_y, last = copies
         from_x[0].wait_recv()
         from_y[0].wait_recv()
         last.start()
@@ -322,6 +327,8 @@
         Y: from_plane,
         V: lambda k: gather_rest(u_copies(k)),
         AS: factors,
+        RQ: lambda _: gather_last(g_copies),
+        VQ: lambda k: gather_last(u_copies(k)),
     }
 
     @pl.loop(0, len(EVENTS))

time: 188 us -> 172 us (0.915)
  the two profiles are of different devices: /device:TPU:0 before, /device:TPU:25 now
where the time goes in v2:
time: 172 us
  Pallas kernels  160 us (93%)
  local copies, waits for them, and re-layouts  11.6 us (7%)
    pallas_call x1, Pallas kernels, device_step(): pl.pallas_call(kernel, out_shape=(jax.ShapeDtypeStruct((LAYERS * 8, 2, CO...  150 us
    unnamed x11, local copies, waits for them, and re-layouts  9.57 us
    pallas_call x1, Pallas kernels, device_step(): pl.pallas_call(open_rows, out_shape=jax.ShapeDtypeStruct((LAYERS, D, D),...  9.5 us

profile of v2, /device:TPU:25, one launch (start us, length us, event | category | flops | bytes accessed | tf_op | source)
XLA Modules:
  0.0 172.0 jit_solution(13217951782260239035)
XLA Ops:
  0.6 0.0 copy-start
  0.6 2.8 %copy.10 = bf16[1024,768]{0,1:T(8,128)(2,1)} copy(bf16[1024,768]{1,0:T(8,128)(2,1)} %param.7) | data formatting | bytes 3145728 | tf_op args[0]
  3.4 0.0 copy-done
  3.4 1.7 copy.11
  5.1 0.0 slice-start
  5.1 2.0 %slice-done = bf16[3,768,768]{2,1,0:T(8,128)(2,1)S(1)} async-done(((bf16[4,768,768]{2,1,0:T(8,128)(2,1)}), bf16[3,768,768]{2,1,0:T(8,128)(2,1)S(1)}, s32[]{:S(2)}) %slice-start) | async-done | bytes 3538968 | tf_op jit(solution)/shard_map/slice | solution.py:419
  7.1 3.7 %copy.13 = bf16[3,768,768]{1,2,0:T(8,128)(2,1)} copy(bf16[3,768,768]{2,1,0:T(8,128)(2,1)S(1)} %slice-done) | data formatting | bytes 7077888
  10.8 150.2 %shard_map.94 = (bf16[32,2,144,384]{3,2,1,0:T(8,128)(2,1)}, f32[96,768]{1,0:T(8,128)}, f32[96,768]{1,0:T(8,128)}) custom-call(bf16[768,1024]{1,0:T(8,128)(2,1)} %bitcast.4, bf16[768,1024]{1,0:T(8,128)(2,1)} %bitcast.5, bf16[3,768,768]{2,1,0:T(8,128)(2,1)} %bitcast.3, bf16[4,768,768]{2,1,0:T(8,128)(2,1)} %w_hbm.1, f32[4,768,768]{2,1,0:T(8,128)} %sinv_hbm.1, ...), custom_call_target="tpu_custom_call" | custom-call | tf_op jit(solution)/shard_map/pallas_call | solution.py:382
  161.0 0.0 copy-start.2
  161.0 0.0 copy-start.1
  161.0 9.5 %shard_map.95 = f32[4,768,768]{2,1,0:T(8,128)} custom-call(bf16[32,2,144,384]{3,2,1,0:T(8,128)(2,1)} %get-tuple-element.6.code), custom_call_target="tpu_custom_call" | custom-call | tf_op jit(solution)/shard_map/pallas_call | solution.py:420
  170.5 0.0 copy-done.2
  170.5 0.7 copy.16
  171.2 0.0 copy-done.1
  171.2 0.7 copy.17
Async XLA Ops:
  0.6 2.8 %copy-start = (bf16[1024,768]{1,0:T(8,128)(2,1)S(1)}, bf16[1024,768]{1,0:T(8,128)(2,1)}, u32[]{:S(2)}) copy-start(bf16[1024,768]{1,0:T(8,128)(2,1)} %param.8) | copy-start | bytes 4718596
  5.1 2.0 %slice-start = ((bf16[4,768,768]{2,1,0:T(8,128)(2,1)}), bf16[3,768,768]{2,1,0:T(8,128)(2,1)S(1)}, s32[]{:S(2)}) async-start(bf16[4,768,768]{2,1,0:T(8,128)(2,1)} %w_hbm.1), calls=%async_computation | async-start | bytes 7077888 | tf_op jit(solution)/shard_map/slice | solution.py:419
  161.0 9.5 %copy-start.2 = (f32[96,768]{1,0:T(8,128)S(1)}, f32[96,768]{1,0:T(8,128)}, u32[]{:S(2)}) copy-start(f32[96,768]{1,0:T(8,128)} %get-tuple-element.13) | copy-start | bytes 884740
  161.0 10.2 %copy-start.1 = (f32[96,768]{1,0:T(8,128)S(1)}, f32[96,768]{1,0:T(8,128)}, u32[]{:S(2)}) copy-start(f32[96,768]{1,0:T(8,128)} %get-tuple-element.14) | copy-start | bytes 884740

commit v3 on v2

v3 whole, which is shorter than its diff:
```python
import math
import jax
import jax.numpy as jnp
from jax import lax
from jax.experimental import pallas as pl
from jax.experimental.pallas import tpu as pltpu
from jax.sharding import PartitionSpec as P

DECAY = 0.75
F32 = jnp.float32
BF16 = jnp.bfloat16
MESH = pl.DeviceIdType.MESH
HIGH = lax.Precision.HIGHEST
LAYERS = 4
D = 768
ROWS = 1024
BATCH = 32 * ROWS
OWN = 96
HALF = 384
BAND = 512
BHALF = BAND // 2
GELU_C = math.sqrt(2.0 / math.pi)
NT = (((1,), (1,)), ((), ()))
TN = (((0,), (0,)), ((), ()))

STEPS = 2560.0
BASE = 21.0
PAIR = OWN // 2
CODE = OWN + PAIR


def nearest(v):
    return (v + 12582912.0) - 12582912.0


def encode(v):
    hi = v.astype(BF16)
    h = hi.astype(F32)
    q = nearest(jnp.clip((v - h) / jnp.where(h == 0.0, 1.0, h) * STEPS, -10.0, 10.0))
    lo = q[:PAIR] * BASE + q[PAIR:]
    return hi, lo.astype(BF16)


def decode(hi, lo):
    h = hi.astype(F32)
    w = lo.astype(F32)
    top = nearest(w * (1.0 / BASE))
    q = jnp.concatenate([top, w - BASE * top], axis=-2)
    return h + h * (q * (1.0 / STEPS))


def put(ref, idx, v):
    hi, lo = encode(v)
    ref[(*idx, slice(0, OWN))] = hi
    ref[(*idx, slice(OWN, CODE))] = lo


def get(ref, idx):
    return decode(ref[(*idx, slice(0, OWN))], ref[(*idx, slice(OWN, CODE))])


def gelu_tanh(v):
    return jnp.tanh(GELU_C * (v + 0.044715 * (v * v * v)))


F, B, W, PR, T, C, Z, R, U, Y, V, AS, RQ, VQ, DY = range(15)
EVENTS = [
    (F, 0), (DY, 0), (W, 0), (PR, 4), (W, 7), (PR, 11), (W, 1), (PR, 5), (F, 1), (F, 2), (T, 4),
    (B, 3), (B, 2), (T, 5), (W, 5), (PR, 1), (W, 3), (PR, 3), (C, 5), (W, 2), (W, 6),
    (PR, 2), (T, 1), (B, 1), (T, 3), (W, 4), (PR, 0), (T, 2), (C, 3), (T, 0), (C, 1),
    (PR, 6), (C, 2), (T, 11), (PR, 9), (C, 0), (T, 6), (T, 9), (C, 6), (Z, 0), (C, 11),
    (C, 4), (R, 0), (PR, 8), (PR, 10), (RQ, 0), (U, 0), (T, 10), (PR, 7), (T, 8), (T, 7),
    (C, 10), (Y, 1), (C, 7), (C, 8), (C, 9), (Y, 2), (V, 1), (Y, 3), (V, 2), (V, 0),
    (V, 3), (VQ, 0), (VQ, 2), (VQ, 1), (VQ, 3), (AS, 0),
]


def kernel(
    x_hbm, dy_hbm, w_hbm, sinv_hbm, a_inv,
    u_out, f_sum, f_flip,
    hg, wbuf, lhs, full, accg, accxg, s1g, r1g, r2g, zrg, accs, accxs, s1s, r1s, r2s, zrs, flip, gcode, gfull, sinv, ubuf,
    in_sem, lsem, wsem, d2d_s, d2d_r, s1_s, s1_r, s2_s, s2_r, z_s, z_r, t_s, t_r, g_s, g_r, uz_s, uz_r, u_s, u_r, us_loc,
):
    me = lax.axis_index("data")
    c = me % 2
    x = (me // 2) % 2
    y = (me // 4) % 2
    z = me // 8
    mate = me + 1 - 2 * c
    x_nbr = me + 2 - 4 * x
    y_nbr = me + 4 - 8 * y
    z_peer = [(me + 8 * k) % 32 for k in range(4)]

    def row_block(dy_, dx_):
        return 4 * ((y + dy_) % 2) + 2 * ((x + dx_) % 2) + c

    blocks = [row_block(0, 0), row_block(0, 1), row_block(1, 0), row_block(1, 1)]

    def rcopy(src, dst, ss, rs, dev):
        return pltpu.make_async_remote_copy(
            src_ref=src, dst_ref=dst, send_sem=ss, recv_sem=rs, device_id=(dev,), device_id_type=MESH
        )

    own = pl.ds(0, ROWS)
    far = pl.ds(ROWS, ROWS)
    def stage(i, j, k):
        return (s1g.at[i, j, k] if i < 4 else gcode.at[2 * (i - 4) + k, j]).at[pl.ds(0, 128)]

    def piece(k, i, j):
        src = (x_hbm, dy_hbm)[k].at[pl.ds(128 * i, 128), pl.ds(HALF * j, HALF)]
        return pltpu.make_async_copy(src, stage(i, j, k), in_sem.at[k, i, j])

    ld_si = pltpu.make_async_copy(sinv_hbm.at[z], sinv, lsem)
    for k in range(2):
        for i in range(8):
            for j in range(2):
                piece(k, i, j).start()
    for l in range(3):
        pltpu.make_async_copy(w_hbm.at[l], wbuf.at[l], wsem.at[l]).start()
    ld_si.start()

    barrier = pltpu.get_barrier_semaphore()
    for dev in [z * 8 + (me + k) % 8 for k in range(1, 8)] + z_peer[1:]:
        pl.semaphore_signal(barrier, inc=1, device_id=(dev,), device_id_type=MESH)
    pl.semaphore_wait(barrier, 10)

    def share(n):
        return rcopy(hg.at[n, :, own], hg.at[n, :, far], d2d_s.at[n], d2d_r.at[n], mate)

    def forward(l):
        pltpu.make_async_copy(w_hbm.at[l], wbuf.at[l], wsem.at[l]).wait()

        @pl.loop(0, 3)
        def _(i):
            rows = pl.ds(pl.multiple_of(i * 256, 256), 256)
            pre = lax.dot_general(wbuf[l, :, rows], hg[l, :, own], TN, preferred_element_type=F32).astype(BF16)
            hg[4 + l, rows, own] = pre
            v = pre.astype(F32)
            hg[l + 1, rows, own] = (v * (0.5 * (1.0 + gelu_tanh(v)))).astype(BF16)

        share(l + 1).start()

        @pl.when(l == 0)
        def _():
            pltpu.make_async_copy(w_hbm.at[3], wbuf.at[0], wsem.at[0]).start()

    def backward(l):
        k = l % 3

        @pl.when(l == 3)
        def _():
            pltpu.make_async_copy(w_hbm.at[3], wbuf.at[0], wsem.at[0]).wait()

        @pl.loop(0, 3)
        def _(i):
            rows = pl.ds(pl.multiple_of(i * 256, 256), 256)
            dh = jnp.dot(wbuf[k, rows, :], hg[4 + l, :, own], preferred_element_type=F32).astype(BF16).astype(F32)
            v = hg[3 + l, rows, own].astype(F32)
            t = gelu_tanh(v)
            slope = 0.5 * (1.0 + t) + (0.5 * v) * (1.0 - t * t) * (GELU_C * (1.0 + (3.0 * 0.044715) * (v * v)))
            hg[3 + l, rows, own] = (dh * slope).astype(BF16)

        share(3 + l).start()

    class Red:
        def __init__(self, first, width, acc, accx, s1, r1, r2, zr):
            self.first, self.width = first, width
            self.acc, self.accx, self.s1, self.r1, self.r2, self.zr = acc, accx, s1, r1, r2, zr

        def cols(self, j):
            return pl.ds(j * self.width, self.width)

        def st1(self, m, j):
            k = m - self.first
            return rcopy(self.s1.at[k, j], self.r1.at[k, j], s1_s.at[m, j], s1_r.at[m, j], (x_nbr, y_nbr)[j])

        def st2(self, m, j):
            k = m - self.first
            return rcopy(self.s1.at[k, 0, j], self.r2.at[k, j], s2_s.at[m, j], s2_r.at[m, j], (y_nbr, x_nbr)[j])

        def turn(self, m):
            k = m - self.first
            self.st1(m, 0).wait_send()
            for j in range(2):
                self.st1(m, j).wait_recv()
                put(self.s1, (k, 0, j), self.accx[k, j] + get(self.r1, (k, j, 1)))
                self.st2(m, j).start()
                self.acc[k, :, self.cols(j)] += get(self.r1, (k, j, 0))

        def z_copy(self, m):
            k = m - self.first
            kind = k // 4
            l = m % 4
            slot = (l - z + 3) % 4
            return rcopy(
                self.s1.at[k, 1], self.zr.at[kind, slot], z_s.at[m], z_r.at[m // 4, slot], (me + 8 * (l - z) + 32) % 32
            )

        def across(self, m):
            k = m - self.first
            self.st1(m, 1).wait_send()
            for j in range(2):
                self.st2(m, j).wait_recv()
                total = self.acc[k, :, self.cols(j)] + get(self.r2, (k, j))
                self.acc[k, :, self.cols(j)] = total

                @pl.when(m % 4 != z)
                def _():
                    put(self.s1, (k, 1, j), total)

            @pl.when(m % 4 != z)
            def _():
                self.z_copy(m).start()

        def z_wait(self, kind):
            for k in range(3):
                rcopy(
                    self.s1.at[0, 1], self.zr.at[kind, k], z_s.at[0], z_r.at[kind + self.first // 4, k], z_peer[k + 1]
                ).wait_recv()

        def z_total(self, kind, j):
            t = self.acc[kind * 4 + z, :, self.cols(j)]
            for k in range(3):
                t = t + get(self.zr, (kind, k, j))
            return t

    rg = Red(0, HALF, accg, accxg, s1g, r1g, r2g, zrg)
    rs = Red(4, BHALF, accs, accxs, s1s, r1s, r2s, zrs)

    def product(m):
        kind = m // 4
        l = m % 4
        left = jnp.where(kind == 2, 4 + l, l)
        right = jnp.where(kind == 1, l, 4 + l)
        for d in range(4):
            lhs[pl.ds(OWN * d, OWN), :] = hg[left, pl.ds(pl.multiple_of(blocks[d] * OWN, OWN), OWN), :]

        @pl.loop(0, 2)
        def _(j):
            cols = pl.ds(pl.multiple_of(j * HALF, HALF), HALF)
            full[:, cols] = lax.dot_general(lhs[...], hg[right, cols, :], NT, preferred_element_type=F32)

        def send(red, pieces):
            k = m - red.first
            for j in range(2):
                cols = slice(j * red.width, (j + 1) * red.width)
                near, other = (1, 2) if j == 0 else (2, 1)
                red.acc[k, :, cols] = pieces[0][:, cols]
                put(red.s1, (k, j, 0), pieces[near][:, cols])
                put(red.s1, (k, j, 1), pieces[3][:, cols])
                red.accx[k, j] = pieces[other][:, cols]
                red.st1(m, j).start()

        @pl.when(kind == 0)
        def _():
            send(rg, [full[pl.ds(OWN * d, OWN), :] for d in range(4)])

        @pl.when(kind > 0)
        def _():
            send(rs, [
                pltpu.roll(full[pl.ds(OWN * d, OWN), :], (D - OWN * blocks[d]) % D, 1)[:, :BAND] for d in range(4)
            ])

    def by_kind(name):
        def act(m):
            @pl.when(m < 4)
            def _():
                getattr(rg, name)(m)

            @pl.when(m >= 4)
            def _():
                getattr(rs, name)(m)

        return act

    inv_batch = 1.0 / BATCH

    def gather_copies(ref, base, ss, rs, own_src):
        def at(rb, half=None):
            return ref.at[base + rb] if half is None else ref.at[base + rb, half]

        first = [
            rcopy(own_src, at(blocks[0]), ss.at[0], rs.at[0], x_nbr),
            rcopy(own_src, at(blocks[0]), ss.at[1], rs.at[1], y_nbr),
            rcopy(own_src, at(blocks[0]), ss.at[2], rs.at[2], mate),
        ]
        from_x = [
            rcopy(at(blocks[1], 0), at(blocks[1], 0), ss.at[3], rs.at[3], y_nbr),
            rcopy(at(blocks[1]), at(blocks[1]), ss.at[5], rs.at[5], mate),
        ]
        from_y = [
            rcopy(at(blocks[2], 1), at(blocks[2], 1), ss.at[4], rs.at[4], x_nbr),
            rcopy(at(blocks[2]), at(blocks[2]), ss.at[6], rs.at[6], mate),
        ]
        last = rcopy(at(blocks[3]), at(blocks[3]), ss.at[7], rs.at[7], mate)
        return first, from_x, from_y, last

    def gather_rest(copies):
        first, from_x, from_y, last = copies
        first[0].wait_recv()
        for cp in from_x:
            cp.start()
        first[1].wait_recv()
        for cp in from_y:
            cp.start()

    def gather_last(copies):
        first, from_x, from_y, last = copies
        from_x[0].wait_recv()
        from_y[0].wait_recv()
        last.start()

    def gather_end(copies):
        first, from_x, from_y, last = copies
        for cp in (first[2], from_x[1], from_y[1], last):
            cp.wait_recv()

    def gather_sent(copies):
        first, from_x, from_y, last = copies
        for cp in (*first, *from_x, *from_y, last):
            cp.wait_send()

    g_copies = gather_copies(gcode, 0, g_s, g_r, gcode.at[blocks[0]])

    def u_row(l):
        return u_out.at[l * 8 + blocks[0]]

    def u_copies(k):
        l = (z - k + 4) % 4
        return gather_copies(u_out, l * 8, u_s.at[k], u_r.at[k], u_row(l))

    own_first = gather_copies(u_out, z * 8, u_s.at[0], u_r.at[0], ubuf)[0]
    local = pltpu.make_async_copy(ubuf, u_row(z), us_loc)

    def z_send(k, l):
        return rcopy(ubuf, u_row(l), uz_s.at[k - 1], uz_r.at[k - 1], (me + 8 * k) % 32)

    def own_grad(_):
        rg.z_wait(0)
        for j in range(2):
            put(gcode, (blocks[0], j), rg.z_total(0, j) * inv_batch)
        for cp in g_copies[0]:
            cp.start()

    def precondition(_):
        gather_end(g_copies)

        @pl.loop(0, 8)
        def _(b):
            for j in range(2):
                gfull[pl.ds(pl.multiple_of(b * OWN, OWN), OWN), pl.ds(j * HALF, HALF)] = get(gcode, (b, j))

        ld_si.wait()
        left_prod = jnp.dot(a_inv[...], gfull[...], precision=HIGH, preferred_element_type=F32)
        u_rows = jnp.dot(left_prod, sinv[...], precision=HIGH, preferred_element_type=F32)
        for j in range(2):
            put(ubuf, (j,), u_rows[:, j * HALF : (j + 1) * HALF])
        for k in range(1, 4):
            z_send(k, z).start()
        for cp in own_first:
            cp.start()
        local.start()

    def from_plane(k):
        z_send(k, (z - k + 4) % 4).wait_recv()
        for cp in u_copies(k)[0]:
            cp.start()

    def flip_copy(kind, e):
        return rcopy(
            flip.at[kind, e - 1], f_flip.at[kind, e - 1], t_s.at[kind, e - 1], t_r.at[kind, e - 1],
            z * 8 + (blocks[0] + e) % 8,
        )

    def factors(_):
        for kind in range(2):
            rs.z_wait(kind)
            for j in range(2):
                f_sum[kind, :, rs.cols(j)] = rs.z_total(kind, j)
            turned = f_sum[kind].T
            for e in range(1, 4):
                flip[kind, e - 1, :, pl.ds(0, OWN)] = turned[OWN * e : OWN * (e + 1)]
                flip_copy(kind, e).start()

    def factors_end():
        for kind in range(2):
            for e in range(1, 4):
                flip_copy(kind, e).wait()

    def turn_rows(k, n):
        for i in range(8):
            for j in range(2):
                piece(k, i, j).wait()
                hg[n, pl.ds(j * HALF, HALF), pl.ds(i * 128, 128)] = stage(i, j, k)[...].T

        share(n).start()

    turn_rows(0, 0)

    actions = {
        F: forward,
        B: backward,
        W: lambda n: share(n).wait_recv(),
        PR: product,
        T: by_kind("turn"),
        C: by_kind("across"),
        Z: own_grad,
        R: lambda _: gather_rest(g_copies),
        U: precondition,
        Y: from_plane,
        V: lambda k: gather_rest(u_copies(k)),
        AS: factors,
        RQ: lambda _: gather_last(g_copies),
        VQ: lambda k: gather_last(u_copies(k)),
        DY: lambda _: turn_rows(1, 7),
    }

    @pl.loop(0, len(EVENTS))
    def _(step):
        code = jnp.int32(0)
        for s, (op, arg) in enumerate(EVENTS):
            code = jnp.where(step == s, op * 16 + arg, code)
        op = code // 16
        arg = code % 16
        for o, act in actions.items():

            @pl.when(op == o)
            def _(act=act):
                act(arg)

    @pl.loop(0, 4)
    def _(k):
        gather_end(u_copies(k))
        gather_sent(u_copies(k))

    for k in range(1, 4):
        z_send(k, z).wait_send()
    local.wait()
    gather_sent(g_copies)

    @pl.loop(0, 8)
    def _(n):
        share(n).wait_send()

    factors_end()

    @pl.loop(0, 12)
    def _(m):
        def sent(red):
            for j in range(2):
                red.st2(m, j).wait_send()

            @pl.when(m % 4 != z)
            def _():
                red.z_copy(m).wait_send()

        @pl.when(m < 4)
        def _():
            sent(rg)

        @pl.when(m >= 4)
        def _():
            sent(rs)


PARTS = 8
PER = LAYERS * 8 // PARTS


def finish(code_hbm, a_old, s_old, f_sum, f_flip, rows_hbm, a_new, s_new, code, rows, old, tot, flip, in_sem, out_sem, f_sem):
    def load(i):
        return pltpu.make_async_copy(code_hbm.at[pl.ds(i * PER, PER)], code.at[pl.ds(i * PER, PER)], in_sem.at[i])

    def store(i):
        part = pl.ds(pl.multiple_of(i * PER * OWN, OWN), PER * OWN)
        return pltpu.make_async_copy(rows.at[part], rows_hbm.at[part], out_sem.at[i])

    pairs = ((a_old, a_new), (s_old, s_new))
    moves = [pltpu.make_async_copy(o, old.at[k], f_sem.at[k]) for k, (o, _) in enumerate(pairs)]
    moves.append(pltpu.make_async_copy(f_sum, tot.at[:, :, pl.ds(0, BAND)], f_sem.at[2]))
    moves.append(pltpu.make_async_copy(f_flip, flip, f_sem.at[3]))
    outs = [pltpu.make_async_copy(old.at[k], n, f_sem.at[4 + k]) for k, (_, n) in enumerate(pairs)]
    for cp in moves:
        cp.start()
    for i in range(PARTS):
        load(i).start()
    for cp in moves:
        cp.wait()
    shift = OWN * (lax.axis_index("data") % 8)
    for k in range(2):
        for e in range(1, 4):
            at = D - OWN * e
            tot[k, :, at : at + OWN] = flip[k, e - 1, :, 0:OWN]
        old[k] = DECAY * old[k] + ((1.0 - DECAY) / BATCH) * pltpu.roll(tot[k], shift, 1)
        outs[k].start()

    @pl.loop(0, PARTS)
    def _(i):
        load(i).wait()
        for b in range(PER):
            n = i * PER + b
            for j in range(2):
                rows[pl.ds(pl.multiple_of(n * OWN, OWN), OWN), pl.ds(j * HALF, HALF)] = get(code, (n, j))
        store(i).start()

    for cp in outs:
        cp.wait()
    for i in range(PARTS):
        store(i).wait()


def solution(mesh):
    def device_step(x_loc, dy_loc, weights, a_old_rows, s_old_rows, a_inv_rows, s_inv):
        hbm = pl.BlockSpec(memory_space=pltpu.HBM)
        vmem = pl.BlockSpec(memory_space=pltpu.VMEM)
        dma = pltpu.SemaphoreType.DMA
        u_code, f_sum, f_flip = pl.pallas_call(
            kernel,
            out_shape=(
                jax.ShapeDtypeStruct((LAYERS * 8, 2, CODE, HALF), BF16),
                jax.ShapeDtypeStruct((2, OWN, BAND), F32),
                jax.ShapeDtypeStruct((2, 3, OWN, 128), F32),
            ),
            in_specs=[hbm] * 4 + [vmem],
            out_specs=(hbm, vmem, hbm),
            scratch_shapes=[
                pltpu.VMEM((2 * LAYERS, D, 2 * ROWS), BF16),
                pltpu.VMEM((3, D, D), BF16),
                pltpu.VMEM((4 * OWN, 2 * ROWS), BF16),
                pltpu.VMEM((4 * OWN, D), F32),
                pltpu.VMEM((4, OWN, D), F32),
                pltpu.VMEM((4, 2, OWN, HALF), F32),
                pltpu.VMEM((4, 2, 2, CODE, HALF), BF16),
                pltpu.VMEM((4, 2, 2, CODE, HALF), BF16),
                pltpu.VMEM((4, 2, CODE, HALF), BF16),
                pltpu.VMEM((1, 3, 2, CODE, HALF), BF16),
                pltpu.VMEM((8, OWN, BAND), F32),
                pltpu.VMEM((8, 2, OWN, BHALF), F32),
                pltpu.VMEM((8, 2, 2, CODE, BHALF), BF16),
                pltpu.VMEM((8, 2, 2, CODE, BHALF), BF16),
                pltpu.VMEM((8, 2, CODE, BHALF), BF16),
                pltpu.VMEM((2, 3, 2, CODE, BHALF), BF16),
                pltpu.VMEM((2, 3, OWN, 128), F32),
                pltpu.VMEM((8, 2, CODE, HALF), BF16),
                pltpu.VMEM((D, D), F32),
                pltpu.VMEM((D, D), F32),
                pltpu.VMEM((2, CODE, HALF), BF16),
                dma((2, 8, 2)),
                dma,
                dma((3,)),
                dma((8,)), dma((8,)),
                dma((12, 2)), dma((12, 2)),
                dma((12, 2)), dma((12, 2)),
                dma((12,)), dma((3, 3)),
                dma((2, 3)), dma((2, 3)),
                dma((8,)), dma((8,)),
                dma((3,)), dma((3,)),
                dma((4, 8)), dma((4, 8)),
                dma,
            ],
            compiler_params=pltpu.CompilerParams(
                collective_id=0, has_side_effects=True, vmem_limit_bytes=67_000_000
            ),
        )(x_loc, dy_loc, weights, s_inv, a_inv_rows)
        own_shape = jax.ShapeDtypeStruct((OWN, D), F32)
        u_rows, a_new, s_new = pl.pallas_call(
            finish,
            out_shape=(jax.ShapeDtypeStruct((LAYERS * D, D), F32), own_shape, own_shape),
            in_specs=[hbm] * 5,
            out_specs=(hbm, hbm, hbm),
            scratch_shapes=[
                pltpu.VMEM((LAYERS * 8, 2, CODE, HALF), BF16),
                pltpu.VMEM((LAYERS * D, D), F32),
                pltpu.VMEM((2, OWN, D), F32),
                pltpu.VMEM((2, OWN, D), F32),
                pltpu.VMEM((2, 3, OWN, 128), F32),
                dma((PARTS,)),
                dma((PARTS,)),
                dma((6,)),
            ],
            compiler_params=pltpu.CompilerParams(vmem_limit_bytes=67_000_000),
        )(u_code, a_old_rows, s_old_rows, f_sum, f_flip)
        return u_rows.reshape(LAYERS, D, D), a_new, s_new

    row_spec = P("data", None)
    return jax.shard_map(
        device_step,
        mesh=mesh,
        in_specs=(row_spec, row_spec, P(), row_spec, row_spec, row_spec, P()),
        out_specs=(P(), row_spec, row_spec),
        check_vma=False,
    )
```

time: 172 us -> 169 us (0.983)
  the two profiles are of different devices: /device:TPU:25 before, /device:TPU:0 now
where the time goes in v3:
time: 169 us
  Pallas kernels  168 us (99%)
    pallas_call x1, Pallas kernels, device_step(): pl.pallas_call(kernel, out_shape=(jax.ShapeDtypeStruct((LAYERS * 8, 2, CO...  160 us
    pallas_call x1, Pallas kernels, device_step(): pl.pallas_call(finish, out_shape=(jax.ShapeDtypeStruct((LAYERS * D, D), F...  7.6 us

profile of v3, /device:TPU:0, one launch (start us, length us, event | category | flops | bytes accessed | tf_op | source)
XLA Modules:
  0.0 168.7 jit_solution(11708688806371531402)
XLA Ops:
  0.6 160.5 %shard_map.94 = (bf16[32,2,144,384]{3,2,1,0:T(8,128)(2,1)}, f32[2,96,512]{2,1,0:T(8,128)}, f32[2,3,96,128]{3,2,1,0:T(8,128)}) custom-call(bf16[1024,768]{1,0:T(8,128)(2,1)} %x_hbm.1, bf16[1024,768]{1,0:T(8,128)(2,1)} %dy_hbm.1, bf16[4,768,768]{2,1,0:T(8,128)(2,1)} %w_hbm.1, f32[4,768,768]{2,1,0:T(8,128)} %sinv_hbm.1, f32[96,768]{1,0:T(8,128)} %a_inv.1), custom_call_target="tpu_custom_call" | custom-call | tf_op jit(solution)/shard_map/pallas_call | solution.py:517
  161.1 7.6 %shard_map.95 = (f32[3072,768]{1,0:T(8,128)}, f32[96,768]{1,0:T(8,128)}, f32[96,768]{1,0:T(8,128)}) custom-call(bf16[32,2,144,384]{3,2,1,0:T(8,128)(2,1)} %get-tuple-element.9.code_hbm, f32[96,768]{1,0:T(8,128)} %a_old.1, f32[96,768]{1,0:T(8,128)} %s_old.1, f32[2,96,512]{2,1,0:T(8,128)} %get-tuple-element.10.f_sum, f32[2,3,96,128]{3,2,1,0:T(8,128)} %get-tuple-element.11.f_flip), custom_call_target="tpu_custom_call" | custom-call | tf_op jit(solution)/shard_map/pallas_call | solution.py:566

commit v4 on v3

--- a/solution.py
+++ b/solution.py
@@ -65,13 +65,13 @@
 
 F, B, W, PR, T, C, Z, R, U, Y, V, AS, RQ, VQ, DY = range(15)
 EVENTS = [
-    (F, 0), (DY, 0), (W, 0), (PR, 4), (W, 7), (PR, 11), (W, 1), (PR, 5), (F, 1), (F, 2), (T, 4),
-    (B, 3), (B, 2), (T, 5), (W, 5), (PR, 1), (W, 3), (PR, 3), (C, 5), (W, 2), (W, 6),
-    (PR, 2), (T, 1), (B, 1), (T, 3), (W, 4), (PR, 0), (T, 2), (C, 3), (T, 0), (C, 1),
-    (PR, 6), (C, 2), (T, 11), (PR, 9), (C, 0), (T, 6), (T, 9), (C, 6), (Z, 0), (C, 11),
-    (C, 4), (R, 0), (PR, 8), (PR, 10), (RQ, 0), (U, 0), (T, 10), (PR, 7), (T, 8), (T, 7),
-    (C, 10), (Y, 1), (C, 7), (C, 8), (C, 9), (Y, 2), (V, 1), (Y, 3), (V, 2), (V, 0),
-    (V, 3), (VQ, 0), (VQ, 2), (VQ, 1), (VQ, 3), (AS, 0),
+    (F, 0), (DY, 0), (F, 1), (F, 2), (W, 7), (PR, 11), (B, 3), (W, 3), (PR, 3), (B, 2),
+    (W, 2), (W, 6), (PR, 2), (B, 1), (T, 11), (T, 3), (T, 2), (W, 0), (W, 4), (PR, 0),
+    (C, 3), (PR, 6), (T, 0), (W, 1), (W, 5), (PR, 1), (PR, 5), (C, 0), (C, 2), (T, 1),
+    (PR, 9), (T, 5), (C, 1), (PR, 7), (C, 11), (PR, 10), (Z, 0), (R, 0), (PR, 4), (C, 5),
+    (T, 6), (T, 10), (RQ, 0), (T, 7), (U, 0), (PR, 8), (V, 0), (T, 9), (T, 8), (T, 4),
+    (Y, 3), (C, 4), (C, 6), (Y, 2), (V, 3), (C, 10), (VQ, 0), (Y, 1), (C, 7), (C, 8),
+    (V, 2), (C, 9), (V, 1), (VQ, 1), (VQ, 3), (VQ, 2), (AS, 0),
 ]
 
 

time: 169 us -> 153 us (0.905)
  the two profiles are of different devices: /device:TPU:0 before, /device:TPU:24 now
where the time goes in v4:
time: 153 us
  Pallas kernels  153 us (100%)
    pallas_call x1, Pallas kernels, device_step(): pl.pallas_call(kernel, out_shape=(jax.ShapeDtypeStruct((LAYERS * 8, 2, CO...  145 us
    pallas_call x1, Pallas kernels, device_step(): pl.pallas_call(finish, out_shape=(jax.ShapeDtypeStruct((LAYERS * D, D), F...  7.6 us

profile of v4, /device:TPU:24, one launch (start us, length us, event | category | flops | bytes accessed | tf_op | source)
XLA Modules:
  0.0 153.2 jit_solution(6516503407881350449)
XLA Ops:
  0.6 145.0 %shard_map.94 = (bf16[32,2,144,384]{3,2,1,0:T(8,128)(2,1)}, f32[2,96,512]{2,1,0:T(8,128)}, f32[2,3,96,128]{3,2,1,0:T(8,128)}) custom-call(bf16[1024,768]{1,0:T(8,128)(2,1)} %x_hbm.1, bf16[1024,768]{1,0:T(8,128)(2,1)} %dy_hbm.1, bf16[4,768,768]{2,1,0:T(8,128)(2,1)} %w_hbm.1, f32[4,768,768]{2,1,0:T(8,128)} %sinv_hbm.1, f32[96,768]{1,0:T(8,128)} %a_inv.1), custom_call_target="tpu_custom_call" | custom-call | tf_op jit(solution)/shard_map/pallas_call | solution.py:517
  145.6 7.6 %shard_map.95 = (f32[3072,768]{1,0:T(8,128)}, f32[96,768]{1,0:T(8,128)}, f32[96,768]{1,0:T(8,128)}) custom-call(bf16[32,2,144,384]{3,2,1,0:T(8,128)(2,1)} %get-tuple-element.9.code_hbm, f32[96,768]{1,0:T(8,128)} %a_old.1, f32[96,768]{1,0:T(8,128)} %s_old.1, f32[2,96,512]{2,1,0:T(8,128)} %get-tuple-element.10.f_sum, f32[2,3,96,128]{3,2,1,0:T(8,128)} %get-tuple-element.11.f_flip), custom_call_target="tpu_custom_call" | custom-call | tf_op jit(solution)/shard_map/pallas_call | solution.py:566

commit v5 on v4

--- a/solution.py
+++ b/solution.py
@@ -23,40 +23,54 @@
 NT = (((1,), (1,)), ((), ()))
 TN = (((0,), (0,)), ((), ()))
 
-STEPS = 2560.0
-BASE = 21.0
-PAIR = OWN // 2
-CODE = OWN + PAIR
+STEPS = {2: 2560.0, 3: 768.0}
+BASE = {2: 21.0, 3: 7.0}
+CODE = OWN + OWN // 2
+SCODE = OWN + OWN // 3
 
 
 def nearest(v):
     return (v + 12582912.0) - 12582912.0
 
 
-def encode(v):
+def encode(v, group):
     hi = v.astype(BF16)
     h = hi.astype(F32)
-    q = nearest(jnp.clip((v - h) / jnp.where(h == 0.0, 1.0, h) * STEPS, -10.0, 10.0))
-    lo = q[:PAIR] * BASE + q[PAIR:]
-    return hi, lo.astype(BF16)
-
-
-def decode(hi, lo):
+    bound = STEPS[group] / 256.0
+    q = nearest(jnp.clip((v - h) / jnp.where(h == 0.0, 1.0, h) * STEPS[group], -bound, bound))
+    n = OWN // group
+    word = q[:n]
+    for k in range(1, group):
+        word = word * BASE[group] + q[k * n : (k + 1) * n]
+    return hi, word.astype(BF16)
+
+
+def decode(hi, lo, group):
     h = hi.astype(F32)
     w = lo.astype(F32)
-    top = nearest(w * (1.0 / BASE))
-    q = jnp.concatenate([top, w - BASE * top], axis=-2)
-    return h + h * (q * (1.0 / STEPS))
+    parts = []
+    for k in range(group - 1, 0, -1):
+        unit = BASE[group] ** k
+        parts.append(nearest(w * (1.0 / unit)))
+        w = w - unit * parts[-1]
+    q = jnp.concatenate([*parts, w], axis=-2)
+    return h + h * (q * (1.0 / STEPS[group]))
+
+
+def rows_of(ref):
+    return ref.shape[-2], OWN // (ref.shape[-2] - OWN)
 
 
 def put(ref, idx, v):
-    hi, lo = encode(v)
+    rows, group = rows_of(ref)
+    hi, lo = encode(v, group)
     ref[(*idx, slice(0, OWN))] = hi
-    ref[(*idx, slice(OWN, CODE))] = lo
+    ref[(*idx, slice(OWN, rows))] = lo
 
 
 def get(ref, idx):
-    return decode(ref[(*idx, slice(0, OWN))], ref[(*idx, slice(OWN, CODE))])
+    rows, group = rows_of(ref)
+    return decode(ref[(*idx, slice(0, OWN))], ref[(*idx, slice(OWN, rows))], group)
 
 
 def gelu_tanh(v):
@@ -66,13 +80,16 @@
 F, B, W, PR, T, C, Z, R, U, Y, V, AS, RQ, VQ, DY = range(15)
 EVENTS = [
     (F, 0), (DY, 0), (F, 1), (F, 2), (W, 7), (PR, 11), (B, 3), (W, 3), (PR, 3), (B, 2),
-    (W, 2), (W, 6), (PR, 2), (B, 1), (T, 11), (T, 3), (T, 2), (W, 0), (W, 4), (PR, 0),
-    (C, 3), (PR, 6), (T, 0), (W, 1), (W, 5), (PR, 1), (PR, 5), (C, 0), (C, 2), (T, 1),
-    (PR, 9), (T, 5), (C, 1), (PR, 7), (C, 11), (PR, 10), (Z, 0), (R, 0), (PR, 4), (C, 5),
-    (T, 6), (T, 10), (RQ, 0), (T, 7), (U, 0), (PR, 8), (V, 0), (T, 9), (T, 8), (T, 4),
-    (Y, 3), (C, 4), (C, 6), (Y, 2), (V, 3), (C, 10), (VQ, 0), (Y, 1), (C, 7), (C, 8),
-    (V, 2), (C, 9), (V, 1), (VQ, 1), (VQ, 3), (VQ, 2), (AS, 0),
+    (W, 2), (W, 6), (PR, 2), (B, 1), (W, 1), (W, 5), (PR, 1), (W, 0), (W, 4), (PR, 0),
+    (T, 1), (T, 3), (PR, 5), (T, 0), (C, 1), (T, 2), (PR, 10), (C, 3), (PR, 6), (C, 0),
+    (PR, 7), (PR, 9), (T, 5), (T, 11), (C, 2), (Z, 0), (R, 0), (C, 5), (PR, 8), (T, 7),
+    (RQ, 0), (C, 11), (T, 9), (T, 6), (U, 0), (PR, 4), (T, 8), (V, 0), (T, 4), (C, 6),
+    (T, 10), (Y, 1), (C, 9), (Y, 2), (C, 4), (V, 1), (C, 8), (Y, 3), (C, 10), (V, 2),
+    (C, 7), (VQ, 0), (V, 3), (VQ, 1), (VQ, 2), (AS, 0), (VQ, 3),
 ]
+CODES = [op * 16 + arg for op, arg in EVENTS]
+CODES += [0] * (-len(CODES) % 3)
+PLAN = [a + 256 * b + 65536 * c for a, b, c in zip(CODES[::3], CODES[1::3], CODES[2::3])]
 
 
 def kernel(
@@ -417,9 +434,11 @@
 
     @pl.loop(0, len(EVENTS))
     def _(step):
-        code = jnp.int32(0)
-        for s, (op, arg) in enumerate(EVENTS):
-            code = jnp.where(step == s, op * 16 + arg, code)
+        third, which = step // 3, step % 3
+        word = jnp.int32(0)
+        for w, packed in enumerate(PLAN):
+            word = jnp.where(third == w, packed, word)
+        code = jnp.where(which == 0, word % 256, jnp.where(which == 1, (word // 256) % 256, word // 65536))
         op = code // 16
         arg = code % 16
         for o, act in actions.items():
@@ -536,10 +555,10 @@
                 pltpu.VMEM((1, 3, 2, CODE, HALF), BF16),
                 pltpu.VMEM((8, OWN, BAND), F32),
                 pltpu.VMEM((8, 2, OWN, BHALF), F32),
-                pltpu.VMEM((8, 2, 2, CODE, BHALF), BF16),
-                pltpu.VMEM((8, 2, 2, CODE, BHALF), BF16),
-                pltpu.VMEM((8, 2, CODE, BHALF), BF16),
-                pltpu.VMEM((2, 3, 2, CODE, BHALF), BF16),
+                pltpu.VMEM((8, 2, 2, SCODE, BHALF), BF16),
+                pltpu.VMEM((8, 2, 2, SCODE, BHALF), BF16),
+                pltpu.VMEM((8, 2, SCODE, BHALF), BF16),
+                pltpu.VMEM((2, 3, 2, SCODE, BHALF), BF16),
                 pltpu.VMEM((2, 3, OWN, 128), F32),
                 pltpu.VMEM((8, 2, CODE, HALF), BF16),
                 pltpu.VMEM((D, D), F32),

time: 153 us -> 148 us (0.967)
  the two profiles are of different devices: /device:TPU:24 before, /device:TPU:0 now
where the time goes in v5:
time: 148 us; the launch traced here: 146 us
  Pallas kernels  145 us (98%)
    pallas_call x1, Pallas kernels, device_step(): pl.pallas_call(kernel, out_shape=(jax.ShapeDtypeStruct((LAYERS * 8, 2, CO...  138 us
    pallas_call x1, Pallas kernels, device_step(): pl.pallas_call(finish, out_shape=(jax.ShapeDtypeStruct((LAYERS * D, D), F...  7.6 us

profile of v5, /device:TPU:0, one launch (start us, length us, event | category | flops | bytes accessed | tf_op | source)
XLA Modules:
  0.0 145.9 jit_solution(13022504394591035684)
XLA Ops:
  0.6 137.6 %shard_map.94 = (bf16[32,2,144,384]{3,2,1,0:T(8,128)(2,1)}, f32[2,96,512]{2,1,0:T(8,128)}, f32[2,3,96,128]{3,2,1,0:T(8,128)}) custom-call(bf16[1024,768]{1,0:T(8,128)(2,1)} %x_hbm.1, bf16[1024,768]{1,0:T(8,128)(2,1)} %dy_hbm.1, bf16[4,768,768]{2,1,0:T(8,128)(2,1)} %w_hbm.1, f32[4,768,768]{2,1,0:T(8,128)} %sinv_hbm.1, f32[96,768]{1,0:T(8,128)} %a_inv.1), custom_call_target="tpu_custom_call" | custom-call | tf_op jit(solution)/shard_map/pallas_call | solution.py:536
  138.2 7.6 %shard_map.95 = (f32[3072,768]{1,0:T(8,128)}, f32[96,768]{1,0:T(8,128)}, f32[96,768]{1,0:T(8,128)}) custom-call(bf16[32,2,144,384]{3,2,1,0:T(8,128)(2,1)} %get-tuple-element.9.code_hbm, f32[96,768]{1,0:T(8,128)} %a_old.1, f32[96,768]{1,0:T(8,128)} %s_old.1, f32[2,96,512]{2,1,0:T(8,128)} %get-tuple-element.10.f_sum, f32[2,3,96,128]{3,2,1,0:T(8,128)} %get-tuple-element.11.f_flip), custom_call_target="tpu_custom_call" | custom-call | tf_op jit(solution)/shard_map/pallas_call | solution.py:585

commit v6 on v5

--- a/solution.py
+++ b/solution.py
@@ -147,13 +147,10 @@
     def forward(l):
         pltpu.make_async_copy(w_hbm.at[l], wbuf.at[l], wsem.at[l]).wait()
 
-        @pl.loop(0, 3)
-        def _(i):
-            rows = pl.ds(pl.multiple_of(i * 256, 256), 256)
-            pre = lax.dot_general(wbuf[l, :, rows], hg[l, :, own], TN, preferred_element_type=F32).astype(BF16)
-            hg[4 + l, rows, own] = pre
-            v = pre.astype(F32)
-            hg[l + 1, rows, own] = (v * (0.5 * (1.0 + gelu_tanh(v)))).astype(BF16)
+        pre = lax.dot_general(wbuf[l], hg[l, :, own], TN, preferred_element_type=F32).astype(BF16)
+        hg[4 + l, :, own] = pre
+        v = pre.astype(F32)
+        hg[l + 1, :, own] = (v * (0.5 * (1.0 + gelu_tanh(v)))).astype(BF16)
 
         share(l + 1).start()
 
@@ -168,9 +165,9 @@
         def _():
             pltpu.make_async_copy(w_hbm.at[3], wbuf.at[0], wsem.at[0]).wait()
 
-        @pl.loop(0, 3)
+        @pl.loop(0, 2)
         def _(i):
-            rows = pl.ds(pl.multiple_of(i * 256, 256), 256)
+            rows = pl.ds(pl.multiple_of(i * 384, 384), 384)
             dh = jnp.dot(wbuf[k, rows, :], hg[4 + l, :, own], preferred_element_type=F32).astype(BF16).astype(F32)
             v = hg[3 + l, rows, own].astype(F32)
             t = gelu_tanh(v)
@@ -252,10 +249,7 @@
         for d in range(4):
             lhs[pl.ds(OWN * d, OWN), :] = hg[left, pl.ds(pl.multiple_of(blocks[d] * OWN, OWN), OWN), :]
 
-        @pl.loop(0, 2)
-        def _(j):
-            cols = pl.ds(pl.multiple_of(j * HALF, HALF), HALF)
-            full[:, cols] = lax.dot_general(lhs[...], hg[right, cols, :], NT, preferred_element_type=F32)
+        full[...] = lax.dot_general(lhs[...], hg[right], NT, preferred_element_type=F32)
 
         def send(red, pieces):
             k = m - red.first

time: 148 us -> 144 us (0.973)
  the two profiles are of different devices: /device:TPU:0 before, /device:TPU:25 now
where the time goes in v6:
time: 144 us
  Pallas kernels  143 us (99%)
    pallas_call x1, Pallas kernels, device_step(): pl.pallas_call(kernel, out_shape=(jax.ShapeDtypeStruct((LAYERS * 8, 2, CO...  136 us
    pallas_call x1, Pallas kernels, device_step(): pl.pallas_call(finish, out_shape=(jax.ShapeDtypeStruct((LAYERS * D, D), F...  7.6 us

profile of v6, /device:TPU:25, one launch (start us, length us, event | category | flops | bytes accessed | tf_op | source)
XLA Modules:
  0.0 143.9 jit_solution(2404600936668195231)
XLA Ops:
  0.6 135.7 %shard_map.94 = (bf16[32,2,144,384]{3,2,1,0:T(8,128)(2,1)}, f32[2,96,512]{2,1,0:T(8,128)}, f32[2,3,96,128]{3,2,1,0:T(8,128)}) custom-call(bf16[1024,768]{1,0:T(8,128)(2,1)} %x_hbm.1, bf16[1024,768]{1,0:T(8,128)(2,1)} %dy_hbm.1, bf16[4,768,768]{2,1,0:T(8,128)(2,1)} %w_hbm.1, f32[4,768,768]{2,1,0:T(8,128)} %sinv_hbm.1, f32[96,768]{1,0:T(8,128)} %a_inv.1), custom_call_target="tpu_custom_call" | custom-call | tf_op jit(solution)/shard_map/pallas_call | solution.py:530
  136.3 7.6 %shard_map.95 = (f32[3072,768]{1,0:T(8,128)}, f32[96,768]{1,0:T(8,128)}, f32[96,768]{1,0:T(8,128)}) custom-call(bf16[32,2,144,384]{3,2,1,0:T(8,128)(2,1)} %get-tuple-element.9.code_hbm, f32[96,768]{1,0:T(8,128)} %a_old.1, f32[96,768]{1,0:T(8,128)} %s_old.1, f32[2,96,512]{2,1,0:T(8,128)} %get-tuple-element.10.f_sum, f32[2,3,96,128]{3,2,1,0:T(8,128)} %get-tuple-element.11.f_flip), custom_call_target="tpu_custom_call" | custom-call | tf_op jit(solution)/shard_map/pallas_call | solution.py:579
